TPU v7x, 32 devices: a whole 2x2x4 slice. The times are simulated.
32 devices in a mesh: kv: 2 (over x), batch: 16 (over z, y, core).
Axes of the slice: x: 2, y: 2, z: 4, core: 2. Of those that a mesh axis runs over, the one named last changes fastest.
Arguments:
- queries: bfloat16 [64, 32, 128], P(('kv', 'batch')), may hold values from -64 to 64
- prefix_keys: bfloat16 [8192, 8, 128], P('batch', 'kv'), may hold values from -6 to 6
- prefix_values: bfloat16 [8192, 8, 128], P('batch', 'kv'), may hold values from -6 to 6
- suffix_keys: bfloat16 [64, 2048, 8, 128], P('batch', None, 'kv'), may hold values from -6 to 6
- suffix_values: bfloat16 [64, 2048, 8, 128], P('batch', None, 'kv'), may hold values from -6 to 6
- suffix_lengths: int32 [64], P('batch'), may hold values from 512 to 2048, as said below
- slot_sequence: int32 [64], P('batch'), may hold values from 0 to 63, as said below
Outputs:
- attended: bfloat16 [64, 32, 128], P(('kv', 'batch'))
Inputs may be any that keep to these rules, and one draw needn't show every extreme that they name: `suffix_lengths`: some slot holds exactly 2048 live tokens. `slot_sequence`: each sequence's suffix occupies exactly one slot; the 64 / 16 slots of one index of batch hold sequences whose output rows lie on pairwise different indices of batch.
All inputs are finite; a program needn't handle non-finite values.
Results may differ from a plain program's by a relative error of at most 0.007.
Values may be sent and summed in bfloat16 or wider, within the bound.
A program may use at most 64 MiB of HBM per device.

v0:
```python
import jax
import jax.numpy as jnp
from jax import lax
from jax.sharding import PartitionSpec as P

negative_fill = -1e30


def fold_block(state, keys_part, values_part, grouped, scale):
    best, total, accum = state
    scores = (
        jnp.einsum("rkjd,tkd->rkjt", grouped, keys_part, preferred_element_type=jnp.float32) * scale
    )
    new_best = jnp.maximum(best, jnp.max(scores, axis=-1))
    weights = jnp.exp(scores - new_best[..., None])
    total = jnp.sum(weights, axis=-1)
    accum = jnp.einsum(
        "rkjt,tkd->rkjd",
        weights.astype(jnp.bfloat16),
        values_part,
        preferred_element_type=jnp.float32,
    )
    return (new_best, total, accum)


def merge_rows(best, total, accum, row_ids, part_best, part_total, part_acc):
    old_best = best[row_ids]
    new_best = jnp.maximum(old_best, part_best)
    first = jnp.exp(old_best - new_best)
    second = jnp.exp(part_best - new_best)
    best = best.at[row_ids].set(new_best)
    total = total.at[row_ids].set(total[row_ids] * first + part_total * second)
    accum = accum.at[row_ids].set(accum[row_ids] * first[..., None] + part_acc * second[..., None])
    return (best, total, accum)


def shards(
    queries, prefix_keys, prefix_values, suffix_keys, suffix_values, suffix_lengths, slot_sequence
):
    kv_count = lax.axis_size("kv")
    batch_count = lax.axis_size("batch")
    per_device = queries.shape[0]
    head_count = queries.shape[1]
    head_dim = queries.shape[2]
    local_heads = head_count // kv_count
    kv_local = prefix_keys.shape[1]
    group_size = local_heads // kv_local
    scale = head_dim ** (-0.5)
    relayed = lax.all_to_all(queries, "kv", split_axis=1, concat_axis=0, tiled=True)
    gathered = lax.all_gather(relayed, "batch", axis=0, tiled=True)
    batch_total = gathered.shape[0]
    everyone = gathered.reshape(batch_count, kv_count, per_device, local_heads, head_dim)
    everyone = everyone.transpose(1, 0, 2, 3, 4).reshape(batch_total, local_heads, head_dim)
    slots = suffix_keys.shape[0]
    suffix_len = suffix_keys.shape[1]
    slot_queries = jnp.take(everyone, slot_sequence, axis=0).reshape(
        slots, kv_local, group_size, head_dim
    )
    scores = (
        jnp.einsum("skjd,stkd->skjt", slot_queries, suffix_keys, preferred_element_type=jnp.float32)
        * scale
    )
    position = jnp.arange(suffix_len)
    scores = jnp.where(
        position[None, None, None, :] < suffix_lengths[:, None, None, None], scores, negative_fill
    )
    suf_best = jnp.max(scores, axis=-1)
    weights = jnp.exp(scores - suf_best[..., None])
    suf_total = jnp.sum(weights, axis=-1)
    suf_acc = jnp.einsum(
        "skjt,stkd->skjd",
        weights.astype(jnp.bfloat16),
        suffix_values,
        preferred_element_type=jnp.float32,
    )
    grouped_all = everyone.reshape(batch_total, kv_local, group_size, head_dim)
    start_state = (
        jnp.full((batch_total, kv_local, group_size), negative_fill, jnp.float32),
        jnp.zeros((batch_total, kv_local, group_size), jnp.float32),
        jnp.zeros((batch_total, kv_local, group_size, head_dim), jnp.float32),
    )
    best, total, accum = fold_block(start_state, prefix_keys, prefix_values, grouped_all, scale)
    best, total, accum = merge_rows(best, total, accum, slot_sequence, suf_best, suf_total, suf_acc)
    got_acc, got_best, got_total = (
        lax.all_to_all(
            lax.all_to_all(
                accum.reshape(batch_total, 1, local_heads, head_dim),
                "kv",
                split_axis=0,
                concat_axis=2,
                tiled=True,
            ),
            "batch",
            split_axis=0,
            concat_axis=1,
            tiled=True,
        ),
        lax.all_to_all(
            lax.all_to_all(
                best.reshape(batch_total, 1, local_heads),
                "kv",
                split_axis=0,
                concat_axis=2,
                tiled=True,
            ),
            "batch",
            split_axis=0,
            concat_axis=1,
            tiled=True,
        ),
        lax.all_to_all(
            lax.all_to_all(
                total.reshape(batch_total, 1, local_heads),
                "kv",
                split_axis=0,
                concat_axis=2,
                tiled=True,
            ),
            "batch",
            split_axis=0,
            concat_axis=1,
            tiled=True,
        ),
    )
    top = jnp.max(got_best, axis=1)
    factor = jnp.exp(got_best - top[:, None, :])
    denominator = jnp.sum(got_total * factor, axis=1)
    numerator = jnp.sum(got_acc * factor[..., None], axis=1)
    return (numerator / denominator[..., None]).astype(jnp.bfloat16)


def solution(mesh):
    return jax.shard_map(
        shards,
        mesh=mesh,
        in_specs=(
            P(("kv", "batch"), None, None),
            P("batch", "kv", None),
            P("batch", "kv", None),
            P("batch", None, "kv", None),
            P("batch", None, "kv", None),
            P("batch"),
            P("batch"),
        ),
        out_specs=P(("kv", "batch"), None, None),
        check_vma=False,
    )
```

profile of v0, /device:TPU:0, one launch (start us, length us, event | category | flops | bytes accessed | tf_op | source)
XLA Modules:
  0.0 114.2 jit_solution(14936565666871693103)
XLA Ops:
  0.0 1.4 %copy.73 = bf16[2,32,128]{2,0,1:T(2,128)(2,1)} copy(bf16[2,32,128]{2,1,0:T(8,128)(2,1)} %param.7) | data formatting | bytes 32768 | tf_op args[0]
  1.4 4.2 %all-to-all-start = ((bf16[2,32,128]{2,0,1:T(2,128)(2,1)}), bf16[2,32,128]{2,0,1:T(2,128)(2,1)S(1)}, u32[]{:S(2)}, u32[]{:S(2)}) async-start(bf16[2,32,128]{2,0,1:T(2,128)(2,1)} %copy.73), calls=%async_computation | async-start | bytes 32768 | tf_op jit(solution)/shard_map/all_to_all | solution.py:49
  5.6 0.7 compare_select_fusion
  6.3 0.7 compare_and_fusion
  7.0 0.7 iota_compare_fusion
  7.7 1.8 %all-to-all-done = bf16[2,32,128]{2,0,1:T(2,128)(2,1)S(1)} async-done(((bf16[2,32,128]{2,0,1:T(2,128)(2,1)}), bf16[2,32,128]{2,0,1:T(2,128)(2,1)S(1)}, u32[]{:S(2)}, u32[]{:S(2)}) %all-to-all-start) | async-done | bytes 16416 | tf_op jit(solution)/shard_map/all_to_all | solution.py:49
  9.5 22.8 %all_gather.3 = bf16[64,16,128]{2,1,0:T(8,128)(2,1)S(1)} all-gather(bf16[4,16,128]{2,1,0:T(8,128)(2,1)S(1)} %bitcast.81), channel_id=1, replica_groups=mesh['kv'=2,'batch'=16] {'batch'}, dimensions={0}, use_global_device_ids=true | all-gather | bytes 278528 | tf_op jit(solution)/shard_map/all_gather | solution.py:50
  32.6 1.6 %bitcast_reduce_fusion = (f32[64,4,4]{0,2,1:T(4,128)S(1)}, f32[4,512,64,4]{1,2,3,0:T(8,128)S(1)}) fusion(bf16[64,4,4,128]{3,0,2,1:T(8,128)(2,1)S(1)} %bitcast.73, bf16[512,4,128,1]{2,1,0,3:T(4,128)(2,1)} %bitcast.74), kind=kOutput, calls=%fused_computation.14 | convolution fusion | flops 135265280 | bytes 2887680 | tf_op jit(solution)/shard_map/rkjd,tkd->rkjt/dot_general | solution.py:12
  34.3 0.6 fusion.11
  36.8 5.8 %fusion.34 = (f32[4,4,4]{2,1,0:T(4,128)S(1)}, f32[4,4,4,2048]{3,2,1,0:T(4,128)S(1)}) fusion(bf16[4,2048,4,128]{3,2,1,0:T(4,128)(2,1)} %param.10, bf16[4,4,4,128]{3,2,1,0:T(4,128)(2,1)S(1)} %bitcast.95, pred[4]{0:T(512)(128)(4,1)S(1)} %compare_and_fusion, pred[4,2048]{1,0:T(4,128)(4,1)S(1)} %iota_compare_fusion), kind=kOutput, calls=%fused_computation.47 | convolution fusion | flops 33955776 | bytes 8937732 | tf_op jit(solution)/shard_map/skjd,stkd->skjt/dot_general | solution.py:60
  42.9 0.6 scatter_fusion.2
  44.8 0.7 reshape.140
  45.5 3.2 %all-to-all-start.5 = ((f32[2,1,512]{2,1,0:T(1,128)}), f32[2,1,512]{2,1,0:T(1,128)S(1)}, u32[]{:S(2)}, u32[]{:S(2)}) async-start(f32[2,1,512]{2,1,0:T(1,128)} %reshape.140), calls=%async_computation.5 | async-start | bytes 8192 | tf_op jit(solution)/shard_map/all_to_all | solution.py:112
  48.7 0.6 scatter_fusion.1
  50.2 0.7 reshape.138
  50.8 1.7 %all-to-all-done.5 = f32[2,1,512]{2,1,0:T(1,128)S(1)} async-done(((f32[2,1,512]{2,1,0:T(1,128)}), f32[2,1,512]{2,1,0:T(1,128)S(1)}, u32[]{:S(2)}, u32[]{:S(2)}) %all-to-all-start.5) | async-done | bytes 4128 | tf_op jit(solution)/shard_map/all_to_all | solution.py:112
  52.5 3.2 %all-to-all-start.3 = ((f32[2,1,512]{2,1,0:T(1,128)}), f32[2,1,512]{2,1,0:T(1,128)S(1)}, u32[]{:S(2)}, u32[]{:S(2)}) async-start(f32[2,1,512]{2,1,0:T(1,128)} %reshape.138), calls=%async_computation.3 | async-start | bytes 8192 | tf_op jit(solution)/shard_map/all_to_all | solution.py:99
  56.3 1.1 copy.84
  57.5 1.6 %gather_fusion = f32[4,4,4,128]{3,2,1,0:T(4,128)S(1)} fusion(f32[64,4,4,128]{3,2,1,0:T(4,128)} %copy.84, s32[1024]{0:T(1024)S(1)} %pad_clamp_fusion), kind=kCustom, calls=%fused_computation | custom fusion | bytes 65552 | tf_op jit(solution)/shard_map/gather | solution.py:33
  59.9 0.7 copy.100
  60.6 3.5 %all-to-all-start.6 = ((f32[32,1,32]{2,1,0:T(1,128)}), f32[32,1,32]{2,1,0:T(1,128)S(1)}, u32[]{:S(2)}, u32[]{:S(2)}) async-start(f32[32,1,32]{2,1,0:T(1,128)} %copy.100), calls=%async_computation.6 | async-start | bytes 32768 | tf_op jit(solution)/shard_map/all_to_all | solution.py:111
  64.1 4.7 %fusion.16 = f32[4,4,4,128]{3,2,1,0:T(4,128)S(1)} fusion(bf16[4,2048,4,128]{3,2,1,0:T(4,128)(2,1)} %param.11, f32[4,4,4,2048]{3,2,1,0:T(4,128)S(1)} %get-tuple-element.14, f32[4,4,4]{2,1,0:T(4,128)S(1)} %get-tuple-element.13, f32[4,4,4,128]{3,2,1,0:T(4,128)S(1)} %gather_fusion, f32[4,4,4]{2,1,0:T(4,128)S(1)} %bitcast.97, f32[4,4,4]{2,1,0:T(4,128)S(1)} %bitcast.96), kind=kOutput, calls=%fused_computation.20 | convolution fusion | flops 33841152 | bytes 8979200 | tf_op jit(solution)/shard_map/skjt,stkd->skjd/dot_general | solution.py:70
  68.8 1.9 %scatter_fusion = f32[64,4,4,128]{3,2,1,0:T(4,128)} fusion(f32[64,4,4,128]{3,2,1,0:T(4,128)} %copy.84, s32[4]{0:T(128)S(1)} %compare_select_fusion, f32[4,4,4,128]{3,2,1,0:T(4,128)S(1)} %fusion.16), kind=kCustom, calls=%fused_computation.4 | custom fusion | bytes 98320 | tf_op jit(solution)/shard_map/scatter | solution.py:33
  70.7 3.5 %all-to-all-start.1 = ((f32[64,1,16,128]{3,2,1,0:T(8,128)}), f32[64,1,16,128]{3,2,1,0:T(8,128)S(1)}, u32[]{:S(2)}, u32[]{:S(2)}) async-start(f32[64,1,16,128]{3,2,1,0:T(8,128)} %bitcast.14), calls=%async_computation.1 | async-start | bytes 1048576 | tf_op jit(solution)/shard_map/all_to_all | solution.py:86
  75.0 0.7 copy.93
  75.7 7.4 %all-to-all-done.1 = f32[64,1,16,128]{3,2,1,0:T(8,128)S(1)} async-done(((f32[64,1,16,128]{3,2,1,0:T(8,128)}), f32[64,1,16,128]{3,2,1,0:T(8,128)S(1)}, u32[]{:S(2)}, u32[]{:S(2)}) %all-to-all-start.1) | async-done | bytes 524320 | tf_op jit(solution)/shard_map/all_to_all | solution.py:86
  83.2 5.8 %all-to-all-start.4 = ((f32[32,1,32]{2,1,0:T(1,128)}), f32[32,1,32]{2,1,0:T(1,128)S(1)}, u32[]{:S(2)}, u32[]{:S(2)}) async-start(f32[32,1,32]{2,1,0:T(1,128)} %copy.93), calls=%async_computation.4 | async-start | bytes 32768 | tf_op jit(solution)/shard_map/all_to_all | solution.py:98
  89.0 0.9 copy.86
  89.8 5.6 %all-to-all-done.4 = f32[32,1,32]{2,1,0:T(1,128)S(1)} async-done(((f32[32,1,32]{2,1,0:T(1,128)}), f32[32,1,32]{2,1,0:T(1,128)S(1)}, u32[]{:S(2)}, u32[]{:S(2)}) %all-to-all-start.4) | async-done | bytes 4128 | tf_op jit(solution)/shard_map/all_to_all | solution.py:98
  95.5 3.6 %all-to-all-start.2 = ((f32[32,1,32,128]{3,2,1,0:T(8,128)}), f32[32,1,32,128]{3,2,1,0:T(8,128)S(1)}, u32[]{:S(2)}, u32[]{:S(2)}) async-start(f32[32,1,32,128]{3,2,1,0:T(8,128)} %bitcast.18), calls=%async_computation.2 | async-start | bytes 1048576 | tf_op jit(solution)/shard_map/all_to_all | solution.py:85
  99.1 14.2 %all-to-all-done.2 = f32[32,1,32,128]{3,2,1,0:T(8,128)S(1)} async-done(((f32[32,1,32,128]{3,2,1,0:T(8,128)}), f32[32,1,32,128]{3,2,1,0:T(8,128)S(1)}, u32[]{:S(2)}, u32[]{:S(2)}) %all-to-all-start.2) | async-done | bytes 524320 | tf_op jit(solution)/shard_map/all_to_all | solution.py:85
  113.5 0.7 divide_convert_fusion
  (36 shorter events, 7.1 us)
Async XLA Ops:
  0.0 55.7 %copy-start = (bf16[512,4,128]{2,1,0:T(4,128)(2,1)S(1)}, bf16[512,4,128]{2,1,0:T(4,128)(2,1)}, u32[]{:S(2)}) copy-start(bf16[512,4,128]{2,1,0:T(4,128)(2,1)} %param.9) | copy-start | bytes 1572868
  1.4 8.1 %all-to-all-start = ((bf16[2,32,128]{2,0,1:T(2,128)(2,1)}), bf16[2,32,128]{2,0,1:T(2,128)(2,1)S(1)}, u32[]{:S(2)}, u32[]{:S(2)}) async-start(bf16[2,32,128]{2,0,1:T(2,128)(2,1)} %copy.73), calls=%async_computation | async-start | bytes 32768 | tf_op jit(solution)/shard_map/all_to_all | solution.py:49
  45.5 7.0 %all-to-all-start.5 = ((f32[2,1,512]{2,1,0:T(1,128)}), f32[2,1,512]{2,1,0:T(1,128)S(1)}, u32[]{:S(2)}, u32[]{:S(2)}) async-start(f32[2,1,512]{2,1,0:T(1,128)} %reshape.140), calls=%async_computation.5 | async-start | bytes 8192 | tf_op jit(solution)/shard_map/all_to_all | solution.py:112
  52.5 8.0 %all-to-all-start.3 = ((f32[2,1,512]{2,1,0:T(1,128)}), f32[2,1,512]{2,1,0:T(1,128)S(1)}, u32[]{:S(2)}, u32[]{:S(2)}) async-start(f32[2,1,512]{2,1,0:T(1,128)} %reshape.138), calls=%async_computation.3 | async-start | bytes 8192 | tf_op jit(solution)/shard_map/all_to_all | solution.py:99
  60.6 10.2 %all-to-all-start.6 = ((f32[32,1,32]{2,1,0:T(1,128)}), f32[32,1,32]{2,1,0:T(1,128)S(1)}, u32[]{:S(2)}, u32[]{:S(2)}) async-start(f32[32,1,32]{2,1,0:T(1,128)} %copy.100), calls=%async_computation.6 | async-start | bytes 32768 | tf_op jit(solution)/shard_map/all_to_all | solution.py:111
  70.7 12.4 %all-to-all-start.1 = ((f32[64,1,16,128]{3,2,1,0:T(8,128)}), f32[64,1,16,128]{3,2,1,0:T(8,128)S(1)}, u32[]{:S(2)}, u32[]{:S(2)}) async-start(f32[64,1,16,128]{3,2,1,0:T(8,128)} %bitcast.14), calls=%async_computation.1 | async-start | bytes 1048576 | tf_op jit(solution)/shard_map/all_to_all | solution.py:86
  83.2 12.3 %all-to-all-start.4 = ((f32[32,1,32]{2,1,0:T(1,128)}), f32[32,1,32]{2,1,0:T(1,128)S(1)}, u32[]{:S(2)}, u32[]{:S(2)}) async-start(f32[32,1,32]{2,1,0:T(1,128)} %copy.93), calls=%async_computation.4 | async-start | bytes 32768 | tf_op jit(solution)/shard_map/all_to_all | solution.py:98
  95.5 17.8 %all-to-all-start.2 = ((f32[32,1,32,128]{3,2,1,0:T(8,128)}), f32[32,1,32,128]{3,2,1,0:T(8,128)S(1)}, u32[]{:S(2)}, u32[]{:S(2)}) async-start(f32[32,1,32,128]{3,2,1,0:T(8,128)} %bitcast.18), calls=%async_computation.2 | async-start | bytes 1048576 | tf_op jit(solution)/shard_map/all_to_all | solution.py:85
where the time goes:
time: 115 us; the launch traced here: 114 us
  waiting for transfers between devices  30.7 us (27%)
  starting transfers between devices  27 us (23%)
  blocking collectives  22.8 us (20%)
  local copies, waits for them, and re-layouts  14.4 us (13%)
  matrix products  12.6 us (11%)
  other arithmetic  6.31 us (5%)
    all_gather x1, blocking collectives, shards(): gathered = lax.all_gather(relayed, 'batch', axis=0, tiled=True)  22.8 us
    all_to_all x1, waiting for transfers between devices, shards(): lax.all_to_all(lax.all_to_all(accum.reshape(batch_total, 1, local_heads,...  14.2 us
    all_to_all x1, waiting for transfers between devices, shards(): lax.all_to_all(accum.reshape(batch_total, 1, local_heads, head_dim), 'kv'...  7.45 us
    all_to_all x1, starting transfers between devices, shards(): lax.all_to_all(lax.all_to_all(best.reshape(batch_total, 1, local_heads),...  5.81 us
    dot_general x1, matrix products, shards(): jnp.einsum('skjd,stkd->skjt', slot_queries, suffix_keys, preferred_elemen...  5.77 us
    all_to_all x1, waiting for transfers between devices, shards(): lax.all_to_all(lax.all_to_all(best.reshape(batch_total, 1, local_heads),...  5.64 us
    dot_general x1, matrix products, shards(): jnp.einsum('skjt,stkd->skjd', weights.astype(jnp.bfloat16), suffix_values...  4.73 us
    all_to_all x1, starting transfers between devices, shards(): lax.all_to_all(queries, 'kv', split_axis=1, concat_axis=0, tiled=True)  4.23 us
  transfers between devices with their start and end apart: 7, of which 5 were waited for; matrix products, arithmetic and copies ran while one was open for 16% of the time, Pallas kernels for 0%

commit v1 on v0

--- a/solution.py
+++ b/solution.py
@@ -47,7 +47,23 @@
     group_size = local_heads // kv_local
     scale = head_dim ** (-0.5)
     relayed = lax.all_to_all(queries, "kv", split_axis=1, concat_axis=0, tiled=True)
-    gathered = lax.all_gather(relayed, "batch", axis=0, tiled=True)
+
+    def stages_all_guide(message, array_dim):
+        mesh_name = "batch"
+        nodes = lax.axis_size(mesh_name)
+        items = []
+        for idx in range(nodes):
+            items.append((idx, (idx + 1) % nodes))
+        far_arr = [None] * nodes
+        far_arr[nodes - 1] = message
+        for nth in range(nodes - 2, -1, -1):
+            far_arr[nth] = lax.ppermute(far_arr[nth + 1], mesh_name, items)
+        passed = jnp.concatenate(far_arr, axis=array_dim)
+        extra = lax.axis_index(mesh_name)
+        reached = (extra + 1) * message.shape[array_dim]
+        return jnp.roll(passed, reached, axis=array_dim)
+
+    gathered = stages_all_guide(relayed, 0)
     batch_total = gathered.shape[0]
     everyone = gathered.reshape(batch_count, kv_count, per_device, local_heads, head_dim)
     everyone = everyone.transpose(1, 0, 2, 3, 4).reshape(batch_total, local_heads, head_dim)

time: 115 us -> 180 us (1.57)
  waiting for transfers between devices: 30.7 us -> 115 us
  blocking collectives: 22.8 us -> 7.89 us
  starting transfers between devices: 27 us -> 22.9 us
    ppermute x0 -> x15, waiting for transfers between devices: none -> 85.8 us  [stages_all_guide(): far_arr[nth] = lax.ppermute(far_arr[nth + 1], mesh_name, items)]
    all_gather x1 -> x0, blocking collectives: 22.8 us -> none  [shards(): gathered = lax.all_gather(relayed, 'batch', axis=0, tiled=True)]
    all_to_all x0 -> x1, blocking collectives: none -> 7.89 us  [shards(): lax.all_to_all(queries, 'kv', split_axis=1, concat_axis=0, tiled=True)]
    all_to_all x1 -> x0, starting transfers between devices: 4.23 us -> none  [shards(): lax.all_to_all(queries, 'kv', split_axis=1, concat_axis=0, tiled=True)]
  transfers between devices with their start and end apart: 7 -> 21, of which waited for: 5 -> 19; matrix products, arithmetic and copies ran while one was open for 16% -> 11% of each run, Pallas kernels for 0% -> 0%
where the time goes in v1:
time: 180 us; the launch traced here: 179 us
  waiting for transfers between devices  115 us (64%)
  starting transfers between devices  22.9 us (13%)
  local copies, waits for them, and re-layouts  14.2 us (8%)
  matrix products  12.6 us (7%)
  blocking collectives  7.89 us (4%)
  other arithmetic  6.32 us (4%)
    ppermute x15, waiting for transfers between devices, stages_all_guide(): far_arr[nth] = lax.ppermute(far_arr[nth + 1], mesh_name, items)  85.8 us
    all_to_all x1, waiting for transfers between devices, shards(): lax.all_to_all(lax.all_to_all(accum.reshape(batch_total, 1, local_heads,...  14.2 us
    all_to_all x1, blocking collectives, shards(): lax.all_to_all(queries, 'kv', split_axis=1, concat_axis=0, tiled=True)  7.89 us
    all_to_all x1, waiting for transfers between devices, shards(): lax.all_to_all(accum.reshape(batch_total, 1, local_heads, head_dim), 'kv'...  7.45 us
    all_to_all x1, starting transfers between devices, shards(): lax.all_to_all(lax.all_to_all(best.reshape(batch_total, 1, local_heads),...  5.81 us
    dot_general x1, matrix products, shards(): jnp.einsum('skjd,stkd->skjt', slot_queries, suffix_keys, preferred_elemen...  5.78 us
    all_to_all x1, waiting for transfers between devices, shards(): lax.all_to_all(lax.all_to_all(best.reshape(batch_total, 1, local_heads),...  5.65 us
    dot_general x1, matrix products, shards(): jnp.einsum('skjt,stkd->skjd', weights.astype(jnp.bfloat16), suffix_values...  4.66 us
  transfers between devices with their start and end apart: 21, of which 19 were waited for; matrix products, arithmetic and copies ran while one was open for 11% of the time, Pallas kernels for 0%

profile of v1, /device:TPU:0, one launch (start us, length us, event | category | flops | bytes accessed | tf_op | source)
XLA Modules:
  0.0 178.9 jit_solution(13730221630633711597)
XLA Ops:
  0.8 7.9 %all_to_all.126 = bf16[2,32,128]{2,0,1:T(2,128)(2,1)S(1)} all-to-all(bf16[2,32,128]{2,0,1:T(2,128)(2,1)S(1)} %copy.73), channel_id=1, replica_groups=mesh['kv'=2,'batch'=16] {'kv'}, dimensions={1} | all-to-all | bytes 32768 | tf_op jit(solution)/shard_map/all_to_all | solution.py:49
  8.8 5.8 %collective-permute-done = bf16[4,16,128]{2,1,0:T(8,128)(2,1)S(1)} collective-permute-done((bf16[4,16,128]{2,1,0:T(8,128)(2,1)S(1)}, bf16[4,16,128]{2,1,0:T(8,128)(2,1)S(1)}, u32[]{:S(2)}, u32[]{:S(2)}) %collective-permute-start) | collective-permute-done | bytes 16416 | tf_op jit(solution)/shard_map/ppermute | solution.py:60
  14.6 5.9 %collective-permute-done.1 = bf16[4,16,128]{2,1,0:T(8,128)(2,1)S(1)} collective-permute-done((bf16[4,16,128]{2,1,0:T(8,128)(2,1)S(1)}, bf16[4,16,128]{2,1,0:T(8,128)(2,1)S(1)}, u32[]{:S(2)}, u32[]{:S(2)}) %collective-permute-start.1) | collective-permute-done | bytes 16416 | tf_op jit(solution)/shard_map/ppermute | solution.py:60
  20.5 5.9 %collective-permute-done.2 = bf16[4,16,128]{2,1,0:T(8,128)(2,1)S(1)} collective-permute-done((bf16[4,16,128]{2,1,0:T(8,128)(2,1)S(1)}, bf16[4,16,128]{2,1,0:T(8,128)(2,1)S(1)}, u32[]{:S(2)}, u32[]{:S(2)}) %collective-permute-start.2) | collective-permute-done | bytes 16416 | tf_op jit(solution)/shard_map/ppermute | solution.py:60
  26.3 5.9 %collective-permute-done.3 = bf16[4,16,128]{2,1,0:T(8,128)(2,1)S(1)} collective-permute-done((bf16[4,16,128]{2,1,0:T(8,128)(2,1)S(1)}, bf16[4,16,128]{2,1,0:T(8,128)(2,1)S(1)}, u32[]{:S(2)}, u32[]{:S(2)}) %collective-permute-start.3) | collective-permute-done | bytes 16416 | tf_op jit(solution)/shard_map/ppermute | solution.py:60
  32.2 5.9 %collective-permute-done.4 = bf16[4,16,128]{2,1,0:T(8,128)(2,1)S(1)} collective-permute-done((bf16[4,16,128]{2,1,0:T(8,128)(2,1)S(1)}, bf16[4,16,128]{2,1,0:T(8,128)(2,1)S(1)}, u32[]{:S(2)}, u32[]{:S(2)}) %collective-permute-start.4) | collective-permute-done | bytes 16416 | tf_op jit(solution)/shard_map/ppermute | solution.py:60
  38.1 5.9 %collective-permute-done.5 = bf16[4,16,128]{2,1,0:T(8,128)(2,1)S(1)} collective-permute-done((bf16[4,16,128]{2,1,0:T(8,128)(2,1)S(1)}, bf16[4,16,128]{2,1,0:T(8,128)(2,1)S(1)}, u32[]{:S(2)}, u32[]{:S(2)}) %collective-permute-start.5) | collective-permute-done | bytes 16416 | tf_op jit(solution)/shard_map/ppermute | solution.py:60
  43.9 5.9 %collective-permute-done.6 = bf16[4,16,128]{2,1,0:T(8,128)(2,1)S(1)} collective-permute-done((bf16[4,16,128]{2,1,0:T(8,128)(2,1)S(1)}, bf16[4,16,128]{2,1,0:T(8,128)(2,1)S(1)}, u32[]{:S(2)}, u32[]{:S(2)}) %collective-permute-start.6) | collective-permute-done | bytes 16416 | tf_op jit(solution)/shard_map/ppermute | solution.py:60
  49.8 5.9 %collective-permute-done.7 = bf16[4,16,128]{2,1,0:T(8,128)(2,1)S(1)} collective-permute-done((bf16[4,16,128]{2,1,0:T(8,128)(2,1)S(1)}, bf16[4,16,128]{2,1,0:T(8,128)(2,1)S(1)}, u32[]{:S(2)}, u32[]{:S(2)}) %collective-permute-start.7) | collective-permute-done | bytes 16416 | tf_op jit(solution)/shard_map/ppermute | solution.py:60
  55.6 5.9 %collective-permute-done.8 = bf16[4,16,128]{2,1,0:T(8,128)(2,1)S(1)} collective-permute-done((bf16[4,16,128]{2,1,0:T(8,128)(2,1)S(1)}, bf16[4,16,128]{2,1,0:T(8,128)(2,1)S(1)}, u32[]{:S(2)}, u32[]{:S(2)}) %collective-permute-start.8) | collective-permute-done | bytes 16416 | tf_op jit(solution)/shard_map/ppermute | solution.py:60
  61.5 5.9 %collective-permute-done.9 = bf16[4,16,128]{2,1,0:T(8,128)(2,1)S(1)} collective-permute-done((bf16[4,16,128]{2,1,0:T(8,128)(2,1)S(1)}, bf16[4,16,128]{2,1,0:T(8,128)(2,1)S(1)}, u32[]{:S(2)}, u32[]{:S(2)}) %collective-permute-start.9) | collective-permute-done | bytes 16416 | tf_op jit(solution)/shard_map/ppermute | solution.py:60
  67.4 5.9 %collective-permute-done.10 = bf16[4,16,128]{2,1,0:T(8,128)(2,1)S(1)} collective-permute-done((bf16[4,16,128]{2,1,0:T(8,128)(2,1)S(1)}, bf16[4,16,128]{2,1,0:T(8,128)(2,1)S(1)}, u32[]{:S(2)}, u32[]{:S(2)}) %collective-permute-start.10) | collective-permute-done | bytes 16416 | tf_op jit(solution)/shard_map/ppermute | solution.py:60
  74.0 5.1 %collective-permute-done.11 = bf16[4,16,128]{2,1,0:T(8,128)(2,1)S(1)} collective-permute-done((bf16[4,16,128]{2,1,0:T(8,128)(2,1)S(1)}, bf16[4,16,128]{2,1,0:T(8,128)(2,1)S(1)}, u32[]{:S(2)}, u32[]{:S(2)}) %collective-permute-start.11) | collective-permute-done | bytes 16416 | tf_op jit(solution)/shard_map/ppermute | solution.py:60
  79.8 5.2 %collective-permute-done.12 = bf16[4,16,128]{2,1,0:T(8,128)(2,1)S(1)} collective-permute-done((bf16[4,16,128]{2,1,0:T(8,128)(2,1)S(1)}, bf16[4,16,128]{2,1,0:T(8,128)(2,1)S(1)}, u32[]{:S(2)}, u32[]{:S(2)}) %collective-permute-start.12) | collective-permute-done | bytes 16416 | tf_op jit(solution)/shard_map/ppermute | solution.py:60
  85.6 5.2 %collective-permute-done.13 = bf16[4,16,128]{2,1,0:T(8,128)(2,1)S(1)} collective-permute-done((bf16[4,16,128]{2,1,0:T(8,128)(2,1)S(1)}, bf16[4,16,128]{2,1,0:T(8,128)(2,1)S(1)}, u32[]{:S(2)}, u32[]{:S(2)}) %collective-permute-start.13) | collective-permute-done | bytes 16416 | tf_op jit(solution)/shard_map/ppermute | solution.py:60
  90.8 5.8 %collective-permute-done.14 = bf16[4,16,128]{2,1,0:T(8,128)(2,1)S(1)} collective-permute-done((bf16[4,16,128]{2,1,0:T(8,128)(2,1)S(1)}, bf16[4,16,128]{2,1,0:T(8,128)(2,1)S(1)}, u32[]{:S(2)}, u32[]{:S(2)}) %collective-permute-start.14) | collective-permute-done | bytes 16416 | tf_op jit(solution)/shard_map/ppermute | solution.py:60
  100.5 5.8 %fusion.34 = (f32[4,4,4]{2,1,0:T(4,128)S(1)}, f32[4,4,4,2048]{3,2,1,0:T(4,128)S(1)}) fusion(bf16[4,2048,4,128]{3,2,1,0:T(4,128)(2,1)} %param.10, bf16[4,4,4,128]{3,2,1,0:T(4,128)(2,1)S(1)} %bitcast.97, pred[4]{0:T(512)(128)(4,1)S(1)} %compare_and_fusion, pred[4,2048]{1,0:T(4,128)(4,1)S(1)} %iota_compare_fusion), kind=kOutput, calls=%fused_computation.80 | convolution fusion | flops 33955776 | bytes 8937732 | tf_op jit(solution)/shard_map/skjd,stkd->skjt/dot_general | solution.py:76
  109.3 3.2 %all-to-all-start.5 = ((f32[2,1,512]{2,1,0:T(1,128)}), f32[2,1,512]{2,1,0:T(1,128)S(1)}, u32[]{:S(2)}, u32[]{:S(2)}) async-start(f32[2,1,512]{2,1,0:T(1,128)} %reshape.140), calls=%async_computation.5 | async-start | bytes 8192 | tf_op jit(solution)/shard_map/all_to_all | solution.py:128
  114.6 1.7 all-to-all-done.5
  116.3 3.2 %all-to-all-start.3 = ((f32[2,1,512]{2,1,0:T(1,128)}), f32[2,1,512]{2,1,0:T(1,128)S(1)}, u32[]{:S(2)}, u32[]{:S(2)}) async-start(f32[2,1,512]{2,1,0:T(1,128)} %reshape.138), calls=%async_computation.3 | async-start | bytes 8192 | tf_op jit(solution)/shard_map/all_to_all | solution.py:115
  119.5 1.6 convolution_bitcast_fusion
  121.1 1.1 copy.84
  122.2 1.6 gather_fusion
  125.3 3.5 %all-to-all-start.6 = ((f32[32,1,32]{2,1,0:T(1,128)}), f32[32,1,32]{2,1,0:T(1,128)S(1)}, u32[]{:S(2)}, u32[]{:S(2)}) async-start(f32[32,1,32]{2,1,0:T(1,128)} %copy.100), calls=%async_computation.6 | async-start | bytes 32768 | tf_op jit(solution)/shard_map/all_to_all | solution.py:127
  128.9 4.7 %fusion.16 = f32[4,4,4,128]{3,2,1,0:T(4,128)S(1)} fusion(bf16[4,2048,4,128]{3,2,1,0:T(4,128)(2,1)} %param.11, f32[4,4,4,2048]{3,2,1,0:T(4,128)S(1)} %get-tuple-element.14, f32[4,4,4]{2,1,0:T(4,128)S(1)} %get-tuple-element.13, f32[4,4,4,128]{3,2,1,0:T(4,128)S(1)} %gather_fusion, f32[4,4,4]{2,1,0:T(4,128)S(1)} %bitcast.99, f32[4,4,4]{2,1,0:T(4,128)S(1)} %bitcast.98), kind=kOutput, calls=%fused_computation.20 | convolution fusion | flops 33841152 | bytes 8979200 | tf_op jit(solution)/shard_map/skjt,stkd->skjd/dot_general | solution.py:86
  133.5 1.9 %scatter_fusion = f32[64,4,4,128]{3,2,1,0:T(4,128)} fusion(f32[64,4,4,128]{3,2,1,0:T(4,128)} %copy.84, s32[4]{0:T(128)S(1)} %compare_select_fusion, f32[4,4,4,128]{3,2,1,0:T(4,128)S(1)} %fusion.16), kind=kCustom, calls=%fused_computation.4 | custom fusion | bytes 98320 | tf_op jit(solution)/shard_map/scatter | solution.py:33
  135.4 3.5 %all-to-all-start.1 = ((f32[64,1,16,128]{3,2,1,0:T(8,128)}), f32[64,1,16,128]{3,2,1,0:T(8,128)S(1)}, u32[]{:S(2)}, u32[]{:S(2)}) async-start(f32[64,1,16,128]{3,2,1,0:T(8,128)} %bitcast.14), calls=%async_computation.1 | async-start | bytes 1048576 | tf_op jit(solution)/shard_map/all_to_all | solution.py:102
  140.4 7.5 %all-to-all-done.1 = f32[64,1,16,128]{3,2,1,0:T(8,128)S(1)} async-done(((f32[64,1,16,128]{3,2,1,0:T(8,128)}), f32[64,1,16,128]{3,2,1,0:T(8,128)S(1)}, u32[]{:S(2)}, u32[]{:S(2)}) %all-to-all-start.1) | async-done | bytes 524320 | tf_op jit(solution)/shard_map/all_to_all | solution.py:102
  147.9 5.8 %all-to-all-start.4 = ((f32[32,1,32]{2,1,0:T(1,128)}), f32[32,1,32]{2,1,0:T(1,128)S(1)}, u32[]{:S(2)}, u32[]{:S(2)}) async-start(f32[32,1,32]{2,1,0:T(1,128)} %copy.93), calls=%async_computation.4 | async-start | bytes 32768 | tf_op jit(solution)/shard_map/all_to_all | solution.py:114
  154.5 5.7 %all-to-all-done.4 = f32[32,1,32]{2,1,0:T(1,128)S(1)} async-done(((f32[32,1,32]{2,1,0:T(1,128)}), f32[32,1,32]{2,1,0:T(1,128)S(1)}, u32[]{:S(2)}, u32[]{:S(2)}) %all-to-all-start.4) | async-done | bytes 4128 | tf_op jit(solution)/shard_map/all_to_all | solution.py:114
  160.2 3.6 %all-to-all-start.2 = ((f32[32,1,32,128]{3,2,1,0:T(8,128)}), f32[32,1,32,128]{3,2,1,0:T(8,128)S(1)}, u32[]{:S(2)}, u32[]{:S(2)}) async-start(f32[32,1,32,128]{3,2,1,0:T(8,128)} %bitcast.18), calls=%async_computation.2 | async-start | bytes 1048576 | tf_op jit(solution)/shard_map/all_to_all | solution.py:101
  163.8 14.2 %all-to-all-done.2 = f32[32,1,32,128]{3,2,1,0:T(8,128)S(1)} async-done(((f32[32,1,32,128]{3,2,1,0:T(8,128)}), f32[32,1,32,128]{3,2,1,0:T(8,128)S(1)}, u32[]{:S(2)}, u32[]{:S(2)}) %all-to-all-start.2) | async-done | bytes 524320 | tf_op jit(solution)/shard_map/all_to_all | solution.py:101
  (97 shorter events, 16.4 us)
Async XLA Ops:
  0.0 97.4 %copy-start = (bf16[512,4,128]{2,1,0:T(4,128)(2,1)S(1)}, bf16[512,4,128]{2,1,0:T(4,128)(2,1)}, u32[]{:S(2)}) copy-start(bf16[512,4,128]{2,1,0:T(4,128)(2,1)} %param.8) | copy-start | bytes 1572868
  8.7 5.9 %collective-permute-start = (bf16[4,16,128]{2,1,0:T(8,128)(2,1)S(1)}, bf16[4,16,128]{2,1,0:T(8,128)(2,1)S(1)}, u32[]{:S(2)}, u32[]{:S(2)}) collective-permute-start(bf16[4,16,128]{2,1,0:T(8,128)(2,1)S(1)} %bitcast.78), channel_id=1, source_target_pairs={{0,1},{1,2},{2,3},{3,4},{4,5},{5,6},{6,7},{7,8},{8,9},{9,10},{10,1... | collective-permute-start | bytes 49160 | tf_op jit(solution)/shard_map/ppermute | solution.py:60
  14.6 5.9 %collective-permute-start.1 = (bf16[4,16,128]{2,1,0:T(8,128)(2,1)S(1)}, bf16[4,16,128]{2,1,0:T(8,128)(2,1)S(1)}, u32[]{:S(2)}, u32[]{:S(2)}) collective-permute-start(bf16[4,16,128]{2,1,0:T(8,128)(2,1)S(1)} %collective-permute-done), channel_id=1, source_target_pairs={{0,1},{1,2},{2,3},{3,4},{4,5},{5,6},{6,7},{7,8},{8,9},{9,10},{10,1... | collective-permute-start | bytes 49160 | tf_op jit(solution)/shard_map/ppermute | solution.py:60
  20.5 5.9 %collective-permute-start.2 = (bf16[4,16,128]{2,1,0:T(8,128)(2,1)S(1)}, bf16[4,16,128]{2,1,0:T(8,128)(2,1)S(1)}, u32[]{:S(2)}, u32[]{:S(2)}) collective-permute-start(bf16[4,16,128]{2,1,0:T(8,128)(2,1)S(1)} %collective-permute-done.1), channel_id=1, source_target_pairs={{0,1},{1,2},{2,3},{3,4},{4,5},{5,6},{6,7},{7,8},{8,9},{9,10},{10,1... | collective-permute-start | bytes 49160 | tf_op jit(solution)/shard_map/ppermute | solution.py:60
  26.3 5.9 %collective-permute-start.3 = (bf16[4,16,128]{2,1,0:T(8,128)(2,1)S(1)}, bf16[4,16,128]{2,1,0:T(8,128)(2,1)S(1)}, u32[]{:S(2)}, u32[]{:S(2)}) collective-permute-start(bf16[4,16,128]{2,1,0:T(8,128)(2,1)S(1)} %collective-permute-done.2), channel_id=1, source_target_pairs={{0,1},{1,2},{2,3},{3,4},{4,5},{5,6},{6,7},{7,8},{8,9},{9,10},{10,1... | collective-permute-start | bytes 49160 | tf_op jit(solution)/shard_map/ppermute | solution.py:60
  32.2 5.9 %collective-permute-start.4 = (bf16[4,16,128]{2,1,0:T(8,128)(2,1)S(1)}, bf16[4,16,128]{2,1,0:T(8,128)(2,1)S(1)}, u32[]{:S(2)}, u32[]{:S(2)}) collective-permute-start(bf16[4,16,128]{2,1,0:T(8,128)(2,1)S(1)} %collective-permute-done.3), channel_id=1, source_target_pairs={{0,1},{1,2},{2,3},{3,4},{4,5},{5,6},{6,7},{7,8},{8,9},{9,10},{10,1... | collective-permute-start | bytes 49160 | tf_op jit(solution)/shard_map/ppermute | solution.py:60
  38.1 5.9 %collective-permute-start.5 = (bf16[4,16,128]{2,1,0:T(8,128)(2,1)S(1)}, bf16[4,16,128]{2,1,0:T(8,128)(2,1)S(1)}, u32[]{:S(2)}, u32[]{:S(2)}) collective-permute-start(bf16[4,16,128]{2,1,0:T(8,128)(2,1)S(1)} %collective-permute-done.4), channel_id=1, source_target_pairs={{0,1},{1,2},{2,3},{3,4},{4,5},{5,6},{6,7},{7,8},{8,9},{9,10},{10,1... | collective-permute-start | bytes 49160 | tf_op jit(solution)/shard_map/ppermute | solution.py:60
  43.9 5.9 %collective-permute-start.6 = (bf16[4,16,128]{2,1,0:T(8,128)(2,1)S(1)}, bf16[4,16,128]{2,1,0:T(8,128)(2,1)S(1)}, u32[]{:S(2)}, u32[]{:S(2)}) collective-permute-start(bf16[4,16,128]{2,1,0:T(8,128)(2,1)S(1)} %collective-permute-done.5), channel_id=1, source_target_pairs={{0,1},{1,2},{2,3},{3,4},{4,5},{5,6},{6,7},{7,8},{8,9},{9,10},{10,1... | collective-permute-start | bytes 49160 | tf_op jit(solution)/shard_map/ppermute | solution.py:60
  49.8 5.9 %collective-permute-start.7 = (bf16[4,16,128]{2,1,0:T(8,128)(2,1)S(1)}, bf16[4,16,128]{2,1,0:T(8,128)(2,1)S(1)}, u32[]{:S(2)}, u32[]{:S(2)}) collective-permute-start(bf16[4,16,128]{2,1,0:T(8,128)(2,1)S(1)} %collective-permute-done.6), channel_id=1, source_target_pairs={{0,1},{1,2},{2,3},{3,4},{4,5},{5,6},{6,7},{7,8},{8,9},{9,10},{10,1... | collective-permute-start | bytes 49160 | tf_op jit(solution)/shard_map/ppermute | solution.py:60
  55.6 5.9 %collective-permute-start.8 = (bf16[4,16,128]{2,1,0:T(8,128)(2,1)S(1)}, bf16[4,16,128]{2,1,0:T(8,128)(2,1)S(1)}, u32[]{:S(2)}, u32[]{:S(2)}) collective-permute-start(bf16[4,16,128]{2,1,0:T(8,128)(2,1)S(1)} %collective-permute-done.7), channel_id=1, source_target_pairs={{0,1},{1,2},{2,3},{3,4},{4,5},{5,6},{6,7},{7,8},{8,9},{9,10},{10,1... | collective-permute-start | bytes 49160 | tf_op jit(solution)/shard_map/ppermute | solution.py:60
  61.5 5.9 %collective-permute-start.9 = (bf16[4,16,128]{2,1,0:T(8,128)(2,1)S(1)}, bf16[4,16,128]{2,1,0:T(8,128)(2,1)S(1)}, u32[]{:S(2)}, u32[]{:S(2)}) collective-permute-start(bf16[4,16,128]{2,1,0:T(8,128)(2,1)S(1)} %collective-permute-done.8), channel_id=1, source_target_pairs={{0,1},{1,2},{2,3},{3,4},{4,5},{5,6},{6,7},{7,8},{8,9},{9,10},{10,1... | collective-permute-start | bytes 49160 | tf_op jit(solution)/shard_map/ppermute | solution.py:60
  67.4 5.9 %collective-permute-start.10 = (bf16[4,16,128]{2,1,0:T(8,128)(2,1)S(1)}, bf16[4,16,128]{2,1,0:T(8,128)(2,1)S(1)}, u32[]{:S(2)}, u32[]{:S(2)}) collective-permute-start(bf16[4,16,128]{2,1,0:T(8,128)(2,1)S(1)} %collective-permute-done.9), channel_id=1, source_target_pairs={{0,1},{1,2},{2,3},{3,4},{4,5},{5,6},{6,7},{7,8},{8,9},{9,10},{10,1... | collective-permute-start | bytes 49160 | tf_op jit(solution)/shard_map/ppermute | solution.py:60
  73.2 5.9 %collective-permute-start.11 = (bf16[4,16,128]{2,1,0:T(8,128)(2,1)S(1)}, bf16[4,16,128]{2,1,0:T(8,128)(2,1)S(1)}, u32[]{:S(2)}, u32[]{:S(2)}) collective-permute-start(bf16[4,16,128]{2,1,0:T(8,128)(2,1)S(1)} %collective-permute-done.10), channel_id=1, source_target_pairs={{0,1},{1,2},{2,3},{3,4},{4,5},{5,6},{6,7},{7,8},{8,9},{9,10},{10,1... | collective-permute-start | bytes 49160 | tf_op jit(solution)/shard_map/ppermute | solution.py:60
  79.1 5.9 %collective-permute-start.12 = (bf16[4,16,128]{2,1,0:T(8,128)(2,1)S(1)}, bf16[4,16,128]{2,1,0:T(8,128)(2,1)S(1)}, u32[]{:S(2)}, u32[]{:S(2)}) collective-permute-start(bf16[4,16,128]{2,1,0:T(8,128)(2,1)S(1)} %collective-permute-done.11), channel_id=1, source_target_pairs={{0,1},{1,2},{2,3},{3,4},{4,5},{5,6},{6,7},{7,8},{8,9},{9,10},{10,1... | collective-permute-start | bytes 49160 | tf_op jit(solution)/shard_map/ppermute | solution.py:60
  85.0 5.9 %collective-permute-start.13 = (bf16[4,16,128]{2,1,0:T(8,128)(2,1)S(1)}, bf16[4,16,128]{2,1,0:T(8,128)(2,1)S(1)}, u32[]{:S(2)}, u32[]{:S(2)}) collective-permute-start(bf16[4,16,128]{2,1,0:T(8,128)(2,1)S(1)} %collective-permute-done.12), channel_id=1, source_target_pairs={{0,1},{1,2},{2,3},{3,4},{4,5},{5,6},{6,7},{7,8},{8,9},{9,10},{10,1... | collective-permute-start | bytes 49160 | tf_op jit(solution)/shard_map/ppermute | solution.py:60
  90.8 5.9 %collective-permute-start.14 = (bf16[4,16,128]{2,1,0:T(8,128)(2,1)S(1)}, bf16[4,16,128]{2,1,0:T(8,128)(2,1)S(1)}, u32[]{:S(2)}, u32[]{:S(2)}) collective-permute-start(bf16[4,16,128]{2,1,0:T(8,128)(2,1)S(1)} %collective-permute-done.13), channel_id=1, source_target_pairs={{0,1},{1,2},{2,3},{3,4},{4,5},{5,6},{6,7},{7,8},{8,9},{9,10},{10,1... | collective-permute-start | bytes 49160 | tf_op jit(solution)/shard_map/ppermute | solution.py:60
  109.3 7.0 %all-to-all-start.5 = ((f32[2,1,512]{2,1,0:T(1,128)}), f32[2,1,512]{2,1,0:T(1,128)S(1)}, u32[]{:S(2)}, u32[]{:S(2)}) async-start(f32[2,1,512]{2,1,0:T(1,128)} %reshape.140), calls=%async_computation.5 | async-start | bytes 8192 | tf_op jit(solution)/shard_map/all_to_all | solution.py:128
  116.3 9.1 %all-to-all-start.3 = ((f32[2,1,512]{2,1,0:T(1,128)}), f32[2,1,512]{2,1,0:T(1,128)S(1)}, u32[]{:S(2)}, u32[]{:S(2)}) async-start(f32[2,1,512]{2,1,0:T(1,128)} %reshape.138), calls=%async_computation.3 | async-start | bytes 8192 | tf_op jit(solution)/shard_map/all_to_all | solution.py:115
  125.3 10.1 %all-to-all-start.6 = ((f32[32,1,32]{2,1,0:T(1,128)}), f32[32,1,32]{2,1,0:T(1,128)S(1)}, u32[]{:S(2)}, u32[]{:S(2)}) async-start(f32[32,1,32]{2,1,0:T(1,128)} %copy.100), calls=%async_computation.6 | async-start | bytes 32768 | tf_op jit(solution)/shard_map/all_to_all | solution.py:127
  135.4 12.4 %all-to-all-start.1 = ((f32[64,1,16,128]{3,2,1,0:T(8,128)}), f32[64,1,16,128]{3,2,1,0:T(8,128)S(1)}, u32[]{:S(2)}, u32[]{:S(2)}) async-start(f32[64,1,16,128]{3,2,1,0:T(8,128)} %bitcast.14), calls=%async_computation.1 | async-start | bytes 1048576 | tf_op jit(solution)/shard_map/all_to_all | solution.py:102
  147.9 12.3 %all-to-all-start.4 = ((f32[32,1,32]{2,1,0:T(1,128)}), f32[32,1,32]{2,1,0:T(1,128)S(1)}, u32[]{:S(2)}, u32[]{:S(2)}) async-start(f32[32,1,32]{2,1,0:T(1,128)} %copy.93), calls=%async_computation.4 | async-start | bytes 32768 | tf_op jit(solution)/shard_map/all_to_all | solution.py:114
  160.2 17.8 %all-to-all-start.2 = ((f32[32,1,32,128]{3,2,1,0:T(8,128)}), f32[32,1,32,128]{3,2,1,0:T(8,128)S(1)}, u32[]{:S(2)}, u32[]{:S(2)}) async-start(f32[32,1,32,128]{3,2,1,0:T(8,128)} %bitcast.18), calls=%async_computation.2 | async-start | bytes 1048576 | tf_op jit(solution)/shard_map/all_to_all | solution.py:101
